TPU v7x, 32 devices: a whole 2x2x4 slice. The times are simulated.
32 devices in a mesh: leaf: 8 (over z, x), rows: 4 (over y, core).
Axes of the slice: x: 2, y: 2, z: 4, core: 2. Of those that a mesh axis runs over, the one named last changes fastest.
Arguments:
- right_side: float32 [8, 32768], P(None, ('leaf', 'rows')), may hold values from -6 to 6
- diagonal: float32 [32768], P(('leaf', 'rows')), may hold values from 0.5 to 4
- tree_order: int32 [32768], P(('leaf', 'rows')), may hold values from 0 to 32767, as said below
- mid_perm: int32 [8], replicated, may hold values from 0 to 7, each once
- col_factor: bfloat16 [32768, 384], P(('leaf', 'rows')), may hold values from -0.1875 to 0.1875
- mid_factor: bfloat16 [3072, 768], P('leaf', 'rows'), may hold values from -0.15625 to 0.15625
- pre_factor: bfloat16 [3072, 768], P('leaf', 'rows'), may hold values from -0.15625 to 0.15625
- row_factor: bfloat16 [48, 32768], P(None, ('leaf', 'rows')), may hold values from -0.875 to 0.875
Outputs:
- solution: float32 [8, 32768], P(None, ('leaf', 'rows'))
- residual: float32 [8, 32768], P(None, ('leaf', 'rows'))
Inputs may be any that keep to these rules, and one draw needn't show every extreme that they name: `tree_order`: each aligned run of 1024 entries, the run starting at b * 1024, is a permutation of b * 1024 to (b + 1) * 1024 - 1. `mid_perm`: a permutation of 0 to 7.
All inputs are finite; a program needn't handle non-finite values.
Results may differ from a plain program's by a relative error of at most 0.025.
Values may be sent and summed in bfloat16 or wider, within the bound.
A program may use at most 64 MiB of HBM per device.

v0:
```python
import jax
import jax.numpy as jnp
from jax import lax
from jax.sharding import PartitionSpec as P

ITERS = 2


def curvature(first, second):
    return lax.psum(jnp.sum(first * second, axis=1), ("leaf", "rows"))


def precond_norm(first, second):
    return lax.psum(jnp.sum(first * second, axis=1), ("leaf", "rows"))


def per_device(
    right_side, diagonal, tree_order, mid_perm, col_factor, mid_factor, pre_factor, row_factor
):
    sides, points = right_side.shape
    rank_size = row_factor.shape[0]
    leaves = mid_perm.shape[0]
    row_count = mid_factor.shape[1] // rank_size
    local_index = tree_order % points
    slot_ids = jnp.arange(leaves, dtype=jnp.int32)
    onehot = (mid_perm[:, None] == slot_ids[None, :]).astype(jnp.bfloat16)
    col_split = col_factor.reshape(points, leaves, rank_size)
    own_gram = jnp.dot(row_factor, row_factor.T, preferred_element_type=jnp.float32)
    gram_blocks = lax.all_gather(own_gram[None], "rows", axis=0, tiled=True)

    def gram_apply(field, mid_weight):
        taken_tree = jnp.take(field, local_index, axis=1).astype(jnp.bfloat16)
        coeffs = jnp.einsum(
            "sn,ngk->gsk", taken_tree, col_split, preferred_element_type=jnp.float32
        ).astype(jnp.bfloat16)
        outgoing = jnp.einsum(
            "qg,gsk->qsk", onehot, coeffs, preferred_element_type=jnp.float32
        ).astype(jnp.bfloat16)
        incoming = lax.all_to_all(
            outgoing.reshape(leaves, sides * rank_size),
            "leaf",
            split_axis=0,
            concat_axis=0,
            tiled=True,
        )
        incoming = incoming.reshape(leaves, sides, rank_size)
        weight_split = mid_weight.reshape(leaves, rank_size, row_count * rank_size)
        partial_value = jnp.einsum(
            "lsk,lkm->sm", incoming, weight_split, preferred_element_type=jnp.float32
        )
        totals = lax.psum(partial_value, "rows")
        head_coef = lax.optimization_barrier(totals.astype(jnp.bfloat16)).astype(jnp.float32)
        head_coef = head_coef.reshape(sides, row_count, rank_size)
        gathered = jnp.einsum(
            "sjk,jkm->sjm", head_coef, gram_blocks, precision=lax.Precision.HIGHEST
        )
        gathered = gathered.reshape(sides, row_count * rank_size).astype(jnp.bfloat16)
        returned = jnp.einsum(
            "sm,lkm->lsk", gathered, weight_split, preferred_element_type=jnp.float32
        ).astype(jnp.bfloat16)
        arrived = lax.all_to_all(
            returned.reshape(leaves, sides * rank_size),
            "leaf",
            split_axis=0,
            concat_axis=0,
            tiled=True,
        )
        arrived = arrived.reshape(leaves, sides, rank_size)
        unsent = jnp.einsum(
            "qg,qsk->gsk", onehot, arrived, preferred_element_type=jnp.float32
        ).astype(jnp.bfloat16)
        tree_out = jnp.einsum("gsk,ngk->sn", unsent, col_split, preferred_element_type=jnp.float32)
        return jnp.zeros_like(tree_out).at[:, local_index].set(tree_out)

    def apply_precond(field):
        return field / diagonal[None, :] + gram_apply(field, pre_factor)

    solution = jnp.zeros_like(right_side)
    residual = right_side
    precond = apply_precond(residual)
    direction = precond
    precond_dot = precond_norm(residual, precond)
    for iteration in range(ITERS):
        image = diagonal[None, :] * direction + gram_apply(direction, mid_factor)
        alpha_step = precond_dot / curvature(direction, image)
        solution = solution + alpha_step[:, None] * direction
        residual = residual - alpha_step[:, None] * image
        if iteration + 1 < ITERS:
            precond = apply_precond(residual)
            dot_next = precond_norm(residual, precond)
            direction = precond + (dot_next / precond_dot)[:, None] * direction
            precond_dot = dot_next
    return (solution, residual)


def solution(mesh):
    return jax.shard_map(
        per_device,
        mesh=mesh,
        in_specs=(
            P(None, ("leaf", "rows")),
            P(("leaf", "rows")),
            P(("leaf", "rows")),
            P(),
            P(("leaf", "rows"), None),
            P("leaf", "rows"),
            P("leaf", "rows"),
            P(None, ("leaf", "rows")),
        ),
        out_specs=(P(None, ("leaf", "rows")), P(None, ("leaf", "rows"))),
        check_vma=False,
    )
```

profile of v0, /device:TPU:0, one launch (start us, length us, event | category | flops | bytes accessed | tf_op | source)
XLA Modules:
  0.0 275.6 jit_solution(600486382952462527)
XLA Ops:
  0.6 0.7 compare_and_fusion
  1.4 0.9 copy.167
  2.3 3.2 %gather_fusion = bf16[1024,8]{1,0:T(8,128)(2,1)S(1)} fusion(bf16[8,1024]{0,1:T(8,128)(2,1)S(1)} %copy.167, s32[1024]{0:T(1024)S(1)} %broadcast_clamp_fusion), kind=kCustom, calls=%fused_computation.clone | custom fusion | bytes 36864 | tf_op jit(solution)/shard_map/jit(_take)/gather | solution.py:32
  5.6 1.4 copy.169
  7.1 0.5 fusion
  8.0 0.5 broadcast.102
  8.5 0.7 reduce.8
  9.2 0.7 reshape.246
  9.9 7.3 %all-to-all-start = ((bf16[8,2,192]{2,1,0:T(2,128)(2,1)}), bf16[8,2,192]{2,1,0:T(2,128)(2,1)S(1)}, u32[]{:S(2)}, u32[]{:S(2)}) async-start(bf16[8,2,192]{2,1,0:T(2,128)(2,1)} %reshape.246), calls=%async_computation | async-start | bytes 16384 | tf_op jit(solution)/shard_map/all_to_all | solution.py:39
  17.5 5.3 %all-gather = f32[192,48]{1,0:T(8,128)S(1)} all-gather(f32[48,48]{1,0:T(8,128)S(1)} %fusion.74), channel_id=2, replica_groups=mesh['leaf'=8,'rows'=4] {'rows'}, dimensions={0}, use_global_device_ids=true | all-gather | bytes 46080 | tf_op jit(solution)/shard_map/all_gather | solution.py:29
  22.8 0.9 all-to-all-done
  24.1 6.3 %psum.56 = bf16[8,192]{1,0:T(8,128)(2,1)S(1)} all-reduce(f32[8,192]{1,0:T(8,128)S(1)} %convolution_bitcast_fusion.7), channel_id=1, replica_groups=mesh['leaf'=8,'rows'=4] {'rows'}, use_global_device_ids=true, to_apply=%region_0.2 | all-reduce | flops 1536 | bytes 9216 | tf_op jit(solution)/shard_map/psum | solution.py:51
  31.1 0.7 reduce.9
  31.9 12.3 %all_to_all.80 = bf16[8,2,192]{2,1,0:T(2,128)(2,1)S(1)} all-to-all(bf16[8,2,192]{2,1,0:T(2,128)(2,1)S(1)} %reshape.248), channel_id=1, replica_groups=mesh['leaf'=8,'rows'=4] {'leaf'}, dimensions={0} | all-to-all | bytes 12288 | tf_op jit(solution)/shard_map/all_to_all | solution.py:61
  44.5 0.3 convolution_bitcast_fusion.3
  45.0 3.2 %scatter_custom_fusion = f32[8,1024]{0,1:T(8,128)S(1)} fusion(s32[1024]{0:T(1024)S(1)} %get-tuple-element.16, f32[1024,8]{1,0:T(8,128)S(1)} %copy.180, f32[]{:T(128)} %constant.15.clone.1), kind=kCustom, calls=%fused_computation.54 | custom fusion | bytes 32772 | tf_op jit(solution)/shard_map/scatter | solution.py:73
  48.4 0.6 copy-done.1
  49.2 3.2 %gather_fusion.1 = bf16[1024,8]{1,0:T(8,128)(2,1)S(1)} fusion(bf16[8,1024]{0,1:T(8,128)(2,1)S(1)} %copy.182, s32[1024]{0:T(1024)S(1)} %broadcast_clamp_fusion), kind=kCustom, calls=%fused_computation.1.clone | custom fusion | bytes 36864 | tf_op jit(solution)/shard_map/jit(_take)/gather | solution.py:32
  52.5 0.5 fusion.2
  53.3 0.7 reduce.10
  54.0 0.7 reshape.250
  54.7 3.3 %all-to-all-start.2 = ((bf16[8,2,192]{2,1,0:T(2,128)(2,1)}), bf16[8,2,192]{2,1,0:T(2,128)(2,1)S(1)}, u32[]{:S(2)}, u32[]{:S(2)}) async-start(bf16[8,2,192]{2,1,0:T(2,128)(2,1)} %reshape.250), calls=%async_computation.2 | async-start | bytes 16384 | tf_op jit(solution)/shard_map/all_to_all | solution.py:39
  58.2 6.3 %all-to-all-done.2 = bf16[8,2,192]{2,1,0:T(2,128)(2,1)S(1)} async-done(((bf16[8,2,192]{2,1,0:T(2,128)(2,1)}), bf16[8,2,192]{2,1,0:T(2,128)(2,1)S(1)}, u32[]{:S(2)}, u32[]{:S(2)}) %all-to-all-start.2) | async-done | bytes 6176 | tf_op jit(solution)/shard_map/all_to_all | solution.py:39
  64.9 6.0 %psum.58 = bf16[8,192]{1,0:T(8,128)(2,1)S(1)} all-reduce(f32[8,192]{1,0:T(8,128)S(1)} %convolution_bitcast_fusion.6), channel_id=1, replica_groups=mesh['leaf'=8,'rows'=4] {'rows'}, use_global_device_ids=true, to_apply=%region_4.6 | all-reduce | flops 1536 | bytes 9216 | tf_op jit(solution)/shard_map/psum | solution.py:51
  71.6 0.7 reduce.11
  72.3 8.9 %all_to_all.81 = bf16[8,2,192]{2,1,0:T(2,128)(2,1)S(1)} all-to-all(bf16[8,2,192]{2,1,0:T(2,128)(2,1)S(1)} %reshape.252), channel_id=1, replica_groups=mesh['leaf'=8,'rows'=4] {'leaf'}, dimensions={0} | all-to-all | bytes 12288 | tf_op jit(solution)/shard_map/all_to_all | solution.py:61
  81.6 0.3 convolution_bitcast_fusion.2
  82.0 3.2 %scatter_custom_fusion.1 = f32[8,1024]{0,1:T(8,128)S(1)} fusion(s32[1024]{0:T(1024)S(1)} %get-tuple-element.16, f32[1024,8]{1,0:T(8,128)S(1)} %copy.194, f32[]{:T(128)} %constant.15.clone.1), kind=kCustom, calls=%fused_computation.52 | custom fusion | bytes 32772 | tf_op jit(solution)/shard_map/scatter | solution.py:73
  85.6 38.2 %all-reduce = (f32[8]{0:T(128)S(1)}, f32[8]{0:T(128)S(1)}) all-reduce(f32[8]{0:T(128)S(1)} %get-tuple-element.12, f32[8]{0:T(128)S(1)} %get-tuple-element.11), channel_id=1, replica_groups=mesh['leaf'=8,'rows'=4] {'leaf','rows'}, use_global_device_ids=true, to_apply=%region_3.5 | all-reduce | flops 16 | bytes 128 | tf_op jit(solution)/shard_map/psum | solution.py:14
  124.1 3.2 %gather_fusion.2 = bf16[1024,8]{1,0:T(8,128)(2,1)S(1)} fusion(bf16[8,1024]{0,1:T(8,128)(2,1)S(1)} %copy.196, s32[1024]{0:T(1024)S(1)} %broadcast_clamp_fusion), kind=kCustom, calls=%fused_computation.2.clone | custom fusion | bytes 36864 | tf_op jit(solution)/shard_map/jit(_take)/gather | solution.py:32
  127.4 0.5 fusion.4
  128.2 0.7 reduce.12
  129.0 11.0 %all_to_all.82 = bf16[8,2,192]{2,1,0:T(2,128)(2,1)S(1)} all-to-all(bf16[8,2,192]{2,1,0:T(2,128)(2,1)S(1)} %reshape.254), channel_id=1, replica_groups=mesh['leaf'=8,'rows'=4] {'leaf'}, dimensions={0} | all-to-all | bytes 12288 | tf_op jit(solution)/shard_map/all_to_all | solution.py:39
  140.3 6.1 %psum.60 = bf16[8,192]{1,0:T(8,128)(2,1)S(1)} all-reduce(f32[8,192]{1,0:T(8,128)S(1)} %convolution_bitcast_fusion.5), channel_id=1, replica_groups=mesh['leaf'=8,'rows'=4] {'rows'}, use_global_device_ids=true, to_apply=%region_8.10 | all-reduce | flops 1536 | bytes 9216 | tf_op jit(solution)/shard_map/psum | solution.py:51
  147.1 0.7 reduce.13
  147.8 8.9 %all_to_all.83 = bf16[8,2,192]{2,1,0:T(2,128)(2,1)S(1)} all-to-all(bf16[8,2,192]{2,1,0:T(2,128)(2,1)S(1)} %reshape.256), channel_id=1, replica_groups=mesh['leaf'=8,'rows'=4] {'leaf'}, dimensions={0} | all-to-all | bytes 12288 | tf_op jit(solution)/shard_map/all_to_all | solution.py:61
  157.5 3.4 %scatter_custom_fusion.2 = f32[8,1024]{0,1:T(8,128)S(1)} fusion(s32[1024]{0:T(1024)S(1)} %get-tuple-element.16, f32[1024,8]{1,0:T(8,128)S(1)} %copy.207, f32[]{:T(128)} %constant.15.clone.1), kind=kCustom, calls=%fused_computation.50 | custom fusion | bytes 32772 | tf_op jit(solution)/shard_map/scatter | solution.py:73
  161.2 38.2 %psum.61 = f32[8]{0:T(128)S(1)} all-reduce(f32[8]{0:T(128)S(1)} %multiply_reduce_fusion.1), channel_id=1, replica_groups=mesh['leaf'=8,'rows'=4] {'leaf','rows'}, use_global_device_ids=true, to_apply=%region_11.13 | all-reduce | flops 8 | bytes 64 | tf_op jit(solution)/shard_map/psum | solution.py:14
  199.7 3.2 %gather_fusion.3 = bf16[1024,8]{1,0:T(8,128)(2,1)S(1)} fusion(bf16[8,1024]{0,1:T(8,128)(2,1)S(1)} %copy.209, s32[1024]{0:T(1024)S(1)} %broadcast_clamp_fusion), kind=kCustom, calls=%fused_computation.3.clone | custom fusion | bytes 36864 | tf_op jit(solution)/shard_map/jit(_take)/gather | solution.py:32
  203.0 0.5 fusion.6
  203.8 0.7 reduce.14
  204.6 11.0 %all_to_all.84 = bf16[8,2,192]{2,1,0:T(2,128)(2,1)S(1)} all-to-all(bf16[8,2,192]{2,1,0:T(2,128)(2,1)S(1)} %reshape.258), channel_id=1, replica_groups=mesh['leaf'=8,'rows'=4] {'leaf'}, dimensions={0} | all-to-all | bytes 12288 | tf_op jit(solution)/shard_map/all_to_all | solution.py:39
  216.0 6.1 %psum.62 = bf16[8,192]{1,0:T(8,128)(2,1)S(1)} all-reduce(f32[8,192]{1,0:T(8,128)S(1)} %convolution_bitcast_fusion.4), channel_id=1, replica_groups=mesh['leaf'=8,'rows'=4] {'rows'}, use_global_device_ids=true, to_apply=%region_12.14 | all-reduce | flops 1536 | bytes 9216 | tf_op jit(solution)/shard_map/psum | solution.py:51
  222.7 0.7 reduce.15
  223.5 8.9 %all_to_all.85 = bf16[8,2,192]{2,1,0:T(2,128)(2,1)S(1)} all-to-all(bf16[8,2,192]{2,1,0:T(2,128)(2,1)S(1)} %reshape.260), channel_id=1, replica_groups=mesh['leaf'=8,'rows'=4] {'leaf'}, dimensions={0} | all-to-all | bytes 12288 | tf_op jit(solution)/shard_map/all_to_all | solution.py:61
  233.2 3.2 %scatter_custom_fusion.3 = f32[8,1024]{0,1:T(8,128)S(1)} fusion(s32[1024]{0:T(1024)S(1)} %get-tuple-element.16, f32[1024,8]{1,0:T(8,128)S(1)} %copy.220, f32[]{:T(128)} %constant.15.clone.1), kind=kCustom, calls=%fused_computation.48 | custom fusion | bytes 32772 | tf_op jit(solution)/shard_map/scatter | solution.py:73
  236.7 38.2 %psum.63 = f32[8]{0:T(128)S(1)} all-reduce(f32[8]{0:T(128)S(1)} %multiply_reduce_fusion), channel_id=1, replica_groups=mesh['leaf'=8,'rows'=4] {'leaf','rows'}, use_global_device_ids=true, to_apply=%region_15.17 | all-reduce | flops 8 | bytes 64 | tf_op jit(solution)/shard_map/psum | solution.py:10
  274.9 0.7 multiply_subtract_fusion
  (115 shorter events, 11.5 us)
Async XLA Ops:
  0.6 16.6 %copy-start = (bf16[48,1024]{1,0:T(8,128)(2,1)S(1)}, bf16[48,1024]{1,0:T(8,128)(2,1)}, u32[]{:S(2)}) copy-start(bf16[48,1024]{1,0:T(8,128)(2,1)} %param.17) | copy-start | bytes 294916
  7.1 0.7 copy-start.5
  7.9 9.4 %copy-start.3 = (bf16[384,192]{0,1:T(8,128)(2,1)S(1)}, bf16[384,192]{0,1:T(8,128)(2,1)}, u32[]{:S(2)}) copy-start(bf16[384,192]{0,1:T(8,128)(2,1)} %param.16) | copy-start | bytes 442372
  9.9 13.8 %all-to-all-start = ((bf16[8,2,192]{2,1,0:T(2,128)(2,1)}), bf16[8,2,192]{2,1,0:T(2,128)(2,1)S(1)}, u32[]{:S(2)}, u32[]{:S(2)}) async-start(bf16[8,2,192]{2,1,0:T(2,128)(2,1)} %reshape.246), calls=%async_computation | async-start | bytes 16384 | tf_op jit(solution)/shard_map/all_to_all | solution.py:39
  48.3 0.8 copy-start.1
  48.3 0.8 copy-start.2
  52.5 5.5 %copy-start.4 = (bf16[384,192]{0,1:T(8,128)(2,1)S(1)}, bf16[384,192]{0,1:T(8,128)(2,1)}, u32[]{:S(2)}) copy-start(bf16[384,192]{0,1:T(8,128)(2,1)} %param.15) | copy-start | bytes 442372
  54.7 9.8 %all-to-all-start.2 = ((bf16[8,2,192]{2,1,0:T(2,128)(2,1)}), bf16[8,2,192]{2,1,0:T(2,128)(2,1)S(1)}, u32[]{:S(2)}, u32[]{:S(2)}) async-start(bf16[8,2,192]{2,1,0:T(2,128)(2,1)} %reshape.250), calls=%async_computation.2 | async-start | bytes 16384 | tf_op jit(solution)/shard_map/all_to_all | solution.py:39
where the time goes:
time: 277 us; the launch traced here: 276 us
  blocking collectives  205 us (74%)
  local copies, waits for them, and re-layouts  37.2 us (13%)
  starting transfers between devices  10.6 us (4%)
  other arithmetic  7.88 us (3%)
  waiting for transfers between devices  7.17 us (3%)
  matrix products  6.49 us (2%)
    psum x2, blocking collectives, precond_norm(): return lax.psum(jnp.sum(first * second, axis=1), ('leaf', 'rows'))  76.4 us
    all_to_all x4, blocking collectives, gram_apply(): lax.all_to_all(returned.reshape(leaves, sides * rank_size), 'leaf', split...  38.9 us
    psum x1, blocking collectives, curvature(): return lax.psum(jnp.sum(first * second, axis=1), ('leaf', 'rows'))  38.2 us
    psum x4, blocking collectives, gram_apply(): totals = lax.psum(partial_value, 'rows')  24.5 us
    all_to_all x2, blocking collectives, gram_apply(): lax.all_to_all(outgoing.reshape(leaves, sides * rank_size), 'leaf', split...  21.9 us
    scatter x8, local copies, waits for them, and re-layouts, gram_apply(): return jnp.zeros_like(tree_out).at[:, local_index].set(tree_out)  13.7 us
    gather x8, local copies, waits for them, and re-layouts, gram_apply(): taken_tree = jnp.take(field, local_index, axis=1).astype(jnp.bfloat16)  13.3 us
    all_to_all x2, starting transfers between devices, gram_apply(): lax.all_to_all(outgoing.reshape(leaves, sides * rank_size), 'leaf', split...  10.6 us
  transfers between devices with their start and end apart: 2, of which 2 were waited for; matrix products, arithmetic and copies ran while one was open for 0% of the time, Pallas kernels for 0%

commit v1 on v0

v1 whole, which is shorter than its diff:
```python
import functools

import jax
import jax.numpy as jnp
from jax import lax
from jax.experimental import pallas as pl
from jax.experimental.pallas import tpu as pltpu
from jax.sharding import PartitionSpec as P

ITERS = 2
LANES = 128
HALF = 64
BF = jnp.bfloat16
F32 = jnp.float32
MESH = pl.DeviceIdType.MESH


def dot(a, b):
    return jnp.dot(a, b, preferred_element_type=F32)


def dot_t(a, b):
    return lax.dot_general(a, b, (((1,), (1,)), ((), ())), preferred_element_type=F32)


def iota(shape, dim):
    return lax.broadcasted_iota(jnp.int32, shape, dim)


def split3(x):
    hi = x.astype(BF).astype(F32)
    mid = (x - hi).astype(BF).astype(F32)
    return hi, mid, x - hi - mid


def kernel(
    n_leaf, n_rows, rhs_ref, diag_ref, order_ref, perm_ref, col_ref, mid_ref, pre_ref, row_ref,
    sol_ref, res_ref,
    place_ref, colp_ref, cpf_ref, wf_ref, gwt_ref, gall_ref,
    fs_ref, fr_ref, rr_ref, bs_ref, br_ref,
    g_send, g_recv, f_send, f_recv, r_send, r_recv, b_send, b_recv,
):
    leaf = lax.axis_index("leaf")
    row = lax.axis_index("rows")
    sides, points = rhs_ref.shape
    rank = row_ref.shape[0]
    mid_cols = mid_ref.shape[1]
    nm = gall_ref.shape[2]
    pairs = n_leaf // 2
    width = pairs * LANES
    parity = lax.rem(leaf, 2)
    waits = []

    barrier = pltpu.get_barrier_semaphore()
    for d in range(1, n_leaf):
        pl.semaphore_signal(barrier, inc=1, device_id=(lax.rem(leaf + d, n_leaf), row), device_id_type=MESH)
    for d in range(1, n_rows):
        pl.semaphore_signal(barrier, inc=1, device_id=(leaf, lax.rem(row + d, n_rows)), device_id_type=MESH)

    factor = row_ref[...]
    gram = dot_t(factor, factor)
    own_cols = (iota((rank, nm), 1) == row * rank + iota((rank, nm), 0))
    own_cols = jnp.where(own_cols, 1.0, 0.0).astype(BF)
    gram_hi = gram.astype(BF)
    gram_lo = (gram - gram_hi.astype(F32)).astype(BF)
    gall_ref[row] = dot(gram_hi, own_cols) + dot(gram_lo, own_cols)
    pl.semaphore_wait(barrier, n_leaf + n_rows - 2)
    gram_copies = []
    for d in range(1, n_rows):
        copy = pltpu.make_async_remote_copy(
            src_ref=gall_ref.at[row], dst_ref=gall_ref.at[row],
            send_sem=g_send.at[d], recv_sem=g_recv.at[d],
            device_id=(leaf, lax.rem(row + d, n_rows)), device_id_type=MESH,
        )
        copy.start()
        gram_copies.append(copy)
    waits += gram_copies

    cols = iota((1, width), 1)
    group = cols // HALF
    inner = cols % HALF
    target = jnp.where(inner < rank, inner, -n_leaf * rank)
    for q in range(n_leaf):
        target = target + jnp.where(group == q, perm_ref[q] * rank, 0)
    place_rows = 128 if n_leaf * rank % 128 == 0 else rank

    @pl.loop(0, n_leaf * rank // place_rows)
    def _(i):
        start = pl.multiple_of(i * place_rows, place_rows)
        hit = (iota((place_rows, width), 0) + start) == target
        place_ref[pl.ds(start, place_rows), :] = jnp.where(hit, 1.0, 0.0).astype(BF)

    chunk = 256

    @pl.loop(0, points // chunk)
    def _(i):
        start = pl.multiple_of(i * chunk, chunk)
        colp_ref[pl.ds(start, chunk), :] = dot(col_ref[pl.ds(start, chunk), :], place_ref[...]).astype(BF)

    local_order = order_ref[...] - (leaf * n_rows + row) * points

    @pl.loop(0, points // chunk)
    def _(i):
        start = pl.multiple_of(i * chunk, chunk)
        hit = (iota((chunk, points), 0) + start) == local_order
        cpf_ref[pl.ds(start, chunk), :] = dot(jnp.where(hit, 1.0, 0.0).astype(BF), colp_ref[...]).astype(BF)

    lane = iota((sides, LANES), 1)
    inner_lane = lane % HALF

    def lanes_of(value):
        hi, mid, lo = split3(value)
        zero = jnp.zeros((sides, LANES), F32)
        vec = jnp.where(inner_lane == rank, hi, zero)
        vec = jnp.where(inner_lane == rank + 1, mid, vec)
        return jnp.where(inner_lane == rank + 2, lo, vec)

    def build_weights(which, source_ref):
        wf_ref[which] = jnp.zeros(wf_ref.shape[1:], BF)
        extra_shape = (HALF - rank, nm)
        extra = (iota(extra_shape, 0) < 3) & (iota(extra_shape, 1) == mid_cols)
        extra = jnp.where(extra, 1.0, 0.0).astype(BF)
        for l in range(n_leaf):
            start = l * LANES + parity * HALF
            wf_ref[which, pl.ds(pl.multiple_of(start, 16), rank), 0:mid_cols] = source_ref[l * rank:(l + 1) * rank, :]
            wf_ref[which, pl.ds(pl.multiple_of(start + rank, 16), HALF - rank), :] = extra

    def gram_pieces():
        full = gall_ref[...].reshape(n_rows * rank, nm)
        full = jnp.concatenate([full, jnp.zeros((nm - n_rows * rank, nm), F32)], axis=0)
        hi = full.astype(BF)
        return hi, (full - hi.astype(F32)).astype(BF)

    def build_back(which):
        hi, lo = gram_pieces()

        @pl.loop(0, n_leaf * LANES // chunk)
        def _(i):
            start = pl.multiple_of(i * chunk, chunk)
            part = wf_ref[which, pl.ds(start, chunk), :]
            gwt_ref[which, pl.ds(start, chunk), :] = (dot(part, hi) + dot(part, lo)).astype(BF)

    def apply(a, which, field, local_dot, first_window=None, last_window=None):
        coeffs = dot(field.astype(BF), cpf_ref[...])
        tagged = lanes_of(local_dot)
        for j in range(pairs):
            fs_ref[a, j] = (coeffs[:, j * LANES:(j + 1) * LANES] + tagged).astype(BF)
        forward = []
        for d in range(1, n_leaf):
            to = lax.rem(leaf + d, n_leaf)
            copy = pltpu.make_async_remote_copy(
                src_ref=fs_ref.at[a, to // 2], dst_ref=fr_ref.at[a, leaf],
                send_sem=f_send.at[a, d], recv_sem=f_recv.at[a, d],
                device_id=(to, row), device_id_type=MESH,
            )
            copy.start()
            forward.append(copy)
        fr_ref[a, leaf] = fs_ref[a, leaf // 2]
        if first_window is not None:
            first_window()
        for copy in forward:
            copy.wait_recv()
        incoming = jnp.concatenate([fr_ref[a, l] for l in range(n_leaf)], axis=1)
        rr_ref[a, row] = dot(incoming, wf_ref[which])
        across = []
        for d in range(1, n_rows):
            copy = pltpu.make_async_remote_copy(
                src_ref=rr_ref.at[a, row], dst_ref=rr_ref.at[a, row],
                send_sem=r_send.at[a, d], recv_sem=r_recv.at[a, d],
                device_id=(leaf, lax.rem(row + d, n_rows)), device_id_type=MESH,
            )
            copy.start()
            across.append(copy)
        hi, lo = gram_pieces()
        for copy in across:
            copy.wait_recv()
        totals = rr_ref[a, 0]
        for r in range(1, n_rows):
            totals = totals + rr_ref[a, r]
        head = totals.astype(BF)
        back = dot_t(head, gwt_ref[which])
        energy = jnp.sum(head.astype(F32) * (dot(head, hi) + dot(head, lo)), axis=1, keepdims=True)
        tagged = jnp.where(lane // HALF == parity, lanes_of(energy), 0.0)
        for l in range(n_leaf):
            bs_ref[a, l] = (back[:, l * LANES:(l + 1) * LANES] + tagged).astype(BF)
        backward = []
        for d in range(1, n_leaf):
            to = lax.rem(leaf + d, n_leaf)
            copy = pltpu.make_async_remote_copy(
                src_ref=bs_ref.at[a, to], dst_ref=br_ref.at[a, leaf],
                send_sem=b_send.at[a, d], recv_sem=b_recv.at[a, d],
                device_id=(to, row), device_id_type=MESH,
            )
            copy.start()
            backward.append(copy)
        br_ref[a, leaf] = bs_ref[a, leaf]
        if last_window is not None:
            last_window()
        for copy in backward:
            copy.wait_recv()
        tiles = [br_ref[a, 2 * j].astype(F32) + br_ref[a, 2 * j + 1].astype(F32) for j in range(pairs)]
        energies = functools.reduce(jnp.add, tiles)
        energies = jnp.where((inner_lane >= rank) & (inner_lane < rank + 3), energies, 0.0)
        arrived = jnp.concatenate(tiles, axis=1).astype(BF)
        image = dot_t(arrived, cpf_ref[...])
        total_dot = totals[:, mid_cols:mid_cols + 1] + jnp.sum(energies, axis=1, keepdims=True)
        waits.extend(forward + across + backward)
        return image, total_dot

    diagonal = diag_ref[...]
    residual = rhs_ref[...]

    def prepare_first():
        build_weights(0, pre_ref)
        for copy in gram_copies:
            copy.wait_recv()
        build_back(0)

    def prepare_second():
        build_weights(1, mid_ref)
        build_back(1)

    scaled = residual / diagonal
    mapped, rz = apply(0, 0, residual, jnp.sum(residual * scaled, axis=1, keepdims=True), prepare_first, prepare_second)
    direction = scaled + mapped
    solution = jnp.zeros_like(residual)
    for iteration in range(ITERS):
        scaled = diagonal * direction
        mapped, curved = apply(2 * iteration + 1, 1, direction, jnp.sum(direction * scaled, axis=1, keepdims=True))
        alpha = rz / curved
        solution = solution + alpha * direction
        residual = residual - alpha * (scaled + mapped)
        if iteration + 1 < ITERS:
            scaled = residual / diagonal
            mapped, rz_next = apply(2 * iteration + 2, 0, residual, jnp.sum(residual * scaled, axis=1, keepdims=True))
            direction = scaled + mapped + (rz_next / rz) * direction
            rz = rz_next
    sol_ref[...] = solution
    res_ref[...] = residual
    for copy in waits:
        copy.wait_send()


def per_device(n_leaf, n_rows, right_side, diagonal, tree_order, mid_perm, col_factor, mid_factor, pre_factor, row_factor):
    sides, points = right_side.shape
    rank = row_factor.shape[0]
    mid_cols = mid_factor.shape[1]
    nm = (mid_cols // LANES + 1) * LANES
    pairs = n_leaf // 2
    applies = 2 * ITERS
    vmem = pl.BlockSpec(memory_space=pltpu.VMEM)
    dma = pltpu.SemaphoreType.DMA
    return pl.pallas_call(
        functools.partial(kernel, n_leaf, n_rows),
        out_shape=(
            jax.ShapeDtypeStruct((sides, points), F32),
            jax.ShapeDtypeStruct((sides, points), F32),
        ),
        in_specs=[vmem, vmem, vmem, pl.BlockSpec(memory_space=pltpu.SMEM), vmem, vmem, vmem, vmem],
        out_specs=(vmem, vmem),
        scratch_shapes=[
            pltpu.VMEM((n_leaf * rank, pairs * LANES), BF),
            pltpu.VMEM((points, pairs * LANES), BF),
            pltpu.VMEM((points, pairs * LANES), BF),
            pltpu.VMEM((2, n_leaf * LANES, nm), BF),
            pltpu.VMEM((2, n_leaf * LANES, nm), BF),
            pltpu.VMEM((n_rows, rank, nm), F32),
            pltpu.VMEM((applies, pairs, sides, LANES), BF),
            pltpu.VMEM((applies, n_leaf, sides, LANES), BF),
            pltpu.VMEM((applies, n_rows, sides, nm), F32),
            pltpu.VMEM((applies, n_leaf, sides, LANES), BF),
            pltpu.VMEM((applies, n_leaf, sides, LANES), BF),
            dma((n_rows,)), dma((n_rows,)),
            dma((applies, n_leaf)), dma((applies, n_leaf)),
            dma((applies, n_rows)), dma((applies, n_rows)),
            dma((applies, n_leaf)), dma((applies, n_leaf)),
        ],
        compiler_params=pltpu.CompilerParams(collective_id=0, has_side_effects=True),
    )(
        right_side, diagonal.reshape(1, points), tree_order.reshape(1, points), mid_perm,
        col_factor, mid_factor, pre_factor, row_factor,
    )


def solution(mesh):
    both = ("leaf", "rows")
    return jax.shard_map(
        functools.partial(per_device, mesh.shape["leaf"], mesh.shape["rows"]),
        mesh=mesh,
        in_specs=(
            P(None, both), P(both), P(both), P(), P(both, None),
            P("leaf", "rows"), P("leaf", "rows"), P(None, both),
        ),
        out_specs=(P(None, both), P(None, both)),
        check_vma=False,
    )
```

time: 277 us -> 65.3 us (0.24)
  blocking collectives: 205 us -> 0 us
  Pallas kernels: 0 us -> 59.8 us
  local copies, waits for them, and re-layouts: 37.2 us -> 4.58 us
  starting transfers between devices: 10.6 us -> 0 us
  other arithmetic: 7.88 us -> 0 us
  waiting for transfers between devices: 7.17 us -> 0 us
  matrix products: 6.49 us -> 0 us
    psum x7 -> x0, blocking collectives: 139 us -> none  [the longest x2 76.4 us: precond_norm(): return lax.psum(jnp.sum(first * second, axis=1), ('leaf', 'rows'))]
    all_to_all x6 -> x0, blocking collectives: 60.9 us -> none  [the longest x4 38.9 us: gram_apply(): lax.all_to_all(returned.reshape(leaves, sides * rank_size), 'leaf', split...]
    pallas_call x0 -> x1, Pallas kernels: none -> 59.8 us  [per_device(): pl.pallas_call(functools.partial(kernel, n_leaf, n_rows), out_shape=(jax....]
    scatter x8 -> x0, local copies, waits for them, and re-layouts: 13.7 us -> none  [gram_apply(): return jnp.zeros_like(tree_out).at[:, local_index].set(tree_out)]
    gather x8 -> x0, local copies, waits for them, and re-layouts: 13.3 us -> none  [gram_apply(): taken_tree = jnp.take(field, local_index, axis=1).astype(jnp.bfloat16)]
    all_to_all x2 -> x0, starting transfers between devices: 10.6 us -> none  [gram_apply(): lax.all_to_all(outgoing.reshape(leaves, sides * rank_size), 'leaf', split...]
    all_to_all x2 -> x0, waiting for transfers between devices: 7.17 us -> none  [gram_apply(): lax.all_to_all(outgoing.reshape(leaves, sides * rank_size), 'leaf', split...]
    dot_general x29 -> x0, matrix products: 6.49 us -> none  [the longest x4 1.93 us: gram_apply(): jnp.einsum('sn,ngk->gsk', taken_tree, col_split, preferred_element_type=j...]
  transfers between devices with their start and end apart: 2 -> 0, of which waited for: 2 -> 0; matrix products, arithmetic and copies ran while one was open for 0% -> 0% of each run, Pallas kernels for 0% -> 0%
where the time goes in v1:
time: 65.3 us; the launch traced here: 65 us
  Pallas kernels  59.8 us (92%)
  local copies, waits for them, and re-layouts  4.58 us (7%)
  between operations  0.66 us (1%)
    pallas_call x1, Pallas kernels, per_device(): pl.pallas_call(functools.partial(kernel, n_leaf, n_rows), out_shape=(jax....  59.8 us
    unnamed x8, local copies, waits for them, and re-layouts  4.58 us

profile of v1, /device:TPU:0, one launch (start us, length us, event | category | flops | bytes accessed | tf_op | source)
XLA Modules:
  0.0 65.0 jit_solution(15302087484977332927)
XLA Ops:
  0.6 0.0 copy-start
  0.6 1.7 %copy.10.mid_ref = bf16[384,192]{1,0:T(8,128)(2,1)} copy(bf16[384,192]{0,1:T(8,128)(2,1)} %param.13) | data formatting | bytes 294912 | tf_op args[5]
  2.4 0.0 copy-done
  2.4 0.8 %copy.11.pre_ref = bf16[384,192]{1,0:T(8,128)(2,1)} copy(bf16[384,192]{0,1:T(8,128)(2,1)S(1)} %copy-done) | data formatting | bytes 294912 | tf_op args[6]
  3.2 59.8 %shard_map.95 = (f32[8,1024]{1,0:T(8,128)}, f32[8,1024]{1,0:T(8,128)}) custom-call(f32[8,1024]{1,0:T(8,128)} %rhs_ref.1, f32[1,1024]{1,0:T(1,128)} %bitcast.2, s32[1,1024]{1,0:T(1,128)} %bitcast.3, s32[8]{0:T(128)} %perm_ref.1, bf16[1024,384]{1,0:T(8,128)(2,1)} %col_ref.1, bf16[384,192]{1,0:T(8,128)(2,1)} %copy.10.mid_ref, bf16[384,192]{1,0:T(8,128)(2,1)} %copy.11.pre_ref, ...), custom_call_target="tpu_custom_call" | custom-call | tf_op jit(solution)/shard_map/pallas_call | solution.py:253
  63.0 0.0 copy-start.1
  63.0 1.4 %copy.14 = f32[8,1024]{1,0:T(8,128)} copy(f32[8,1024]{1,0:T(8,128)} %get-tuple-element.4) | data formatting | bytes 65536
  64.4 0.0 copy-done.1
  64.4 0.6 copy.15
Async XLA Ops:
  0.6 1.8 %copy-start = (bf16[384,192]{0,1:T(8,128)(2,1)S(1)}, bf16[384,192]{0,1:T(8,128)(2,1)}, u32[]{:S(2)}) copy-start(bf16[384,192]{0,1:T(8,128)(2,1)} %param.14) | copy-start | bytes 442372
  63.0 1.4 %copy-start.1 = (f32[8,1024]{1,0:T(8,128)S(1)}, f32[8,1024]{1,0:T(8,128)}, u32[]{:S(2)}) copy-start(f32[8,1024]{1,0:T(8,128)} %get-tuple-element.5) | copy-start | bytes 98308

commit v2 on v1

--- a/solution.py
+++ b/solution.py
@@ -13,6 +13,7 @@
 BF = jnp.bfloat16
 F32 = jnp.float32
 MESH = pl.DeviceIdType.MESH
+CHUNK = 512
 
 
 def dot(a, b):
@@ -36,7 +37,7 @@
 def kernel(
     n_leaf, n_rows, rhs_ref, diag_ref, order_ref, perm_ref, col_ref, mid_ref, pre_ref, row_ref,
     sol_ref, res_ref,
-    place_ref, colp_ref, cpf_ref, wf_ref, gwt_ref, gall_ref,
+    place_ref, colp_ref, cpf_ref, cpb_ref, spread_ref, wf_ref, wb_ref, gall_ref, gram_ref,
     fs_ref, fr_ref, rr_ref, bs_ref, br_ref,
     g_send, g_recv, f_send, f_recv, r_send, r_recv, b_send, b_recv,
 ):
@@ -44,7 +45,7 @@
     row = lax.axis_index("rows")
     sides, points = rhs_ref.shape
     rank = row_ref.shape[0]
-    mid_cols = mid_ref.shape[1]
+    mid_cols = mid_ref.shape[0]
     nm = gall_ref.shape[2]
     pairs = n_leaf // 2
     width = pairs * LANES
@@ -64,6 +65,35 @@
     gram_hi = gram.astype(BF)
     gram_lo = (gram - gram_hi.astype(F32)).astype(BF)
     gall_ref[row] = dot(gram_hi, own_cols) + dot(gram_lo, own_cols)
+    cols = iota((1, width), 1)
+    group = cols // HALF
+    inner = cols % HALF
+    target = jnp.where(inner < rank, inner, -n_leaf * rank)
+    for q in range(n_leaf):
+        target = target + jnp.where(group == q, perm_ref[q] * rank, 0)
+    place_rows = 128 if n_leaf * rank % 128 == 0 else rank
+
+    @pl.loop(0, n_leaf * rank // place_rows)
+    def _(i):
+        start = pl.multiple_of(i * place_rows, place_rows)
+        hit = (iota((place_rows, width), 0) + start) == target
+        place_ref[pl.ds(start, place_rows), :] = jnp.where(hit, 1.0, 0.0).astype(BF)
+
+    chunk = min(CHUNK, points)
+
+    @pl.loop(0, points // chunk)
+    def _(i):
+        start = pl.multiple_of(i * chunk, chunk)
+        colp_ref[pl.ds(start, chunk), :] = dot(col_ref[pl.ds(start, chunk), :], place_ref[...]).astype(BF)
+
+    local_order = order_ref[...] - (leaf * n_rows + row) * points
+
+    @pl.loop(0, points // chunk)
+    def _(i):
+        start = pl.multiple_of(i * chunk, chunk)
+        hit = (iota((chunk, points), 0) + start) == local_order
+        cpf_ref[pl.ds(start, chunk), :] = dot(jnp.where(hit, 1.0, 0.0).astype(BF), colp_ref[...]).astype(BF)
+
     pl.semaphore_wait(barrier, n_leaf + n_rows - 2)
     gram_copies = []
     for d in range(1, n_rows):
@@ -76,35 +106,6 @@
         gram_copies.append(copy)
     waits += gram_copies
 
-    cols = iota((1, width), 1)
-    group = cols // HALF
-    inner = cols % HALF
-    target = jnp.where(inner < rank, inner, -n_leaf * rank)
-    for q in range(n_leaf):
-        target = target + jnp.where(group == q, perm_ref[q] * rank, 0)
-    place_rows = 128 if n_leaf * rank % 128 == 0 else rank
-
-    @pl.loop(0, n_leaf * rank // place_rows)
-    def _(i):
-        start = pl.multiple_of(i * place_rows, place_rows)
-        hit = (iota((place_rows, width), 0) + start) == target
-        place_ref[pl.ds(start, place_rows), :] = jnp.where(hit, 1.0, 0.0).astype(BF)
-
-    chunk = 256
-
-    @pl.loop(0, points // chunk)
-    def _(i):
-        start = pl.multiple_of(i * chunk, chunk)
-        colp_ref[pl.ds(start, chunk), :] = dot(col_ref[pl.ds(start, chunk), :], place_ref[...]).astype(BF)
-
-    local_order = order_ref[...] - (leaf * n_rows + row) * points
-
-    @pl.loop(0, points // chunk)
-    def _(i):
-        start = pl.multiple_of(i * chunk, chunk)
-        hit = (iota((chunk, points), 0) + start) == local_order
-        cpf_ref[pl.ds(start, chunk), :] = dot(jnp.where(hit, 1.0, 0.0).astype(BF), colp_ref[...]).astype(BF)
-
     lane = iota((sides, LANES), 1)
     inner_lane = lane % HALF
 
@@ -115,32 +116,39 @@
         vec = jnp.where(inner_lane == rank + 1, mid, vec)
         return jnp.where(inner_lane == rank + 2, lo, vec)
 
+    def build_spread():
+        cols = iota((1, n_leaf * LANES), 1)
+        inner = cols % HALF
+        target = jnp.where((inner < rank) & ((cols % LANES) // HALF == parity), (cols // LANES) * rank + inner, -1)
+
+        @pl.loop(0, n_leaf * rank // place_rows)
+        def _(i):
+            start = pl.multiple_of(i * place_rows, place_rows)
+            hit = (iota((place_rows, n_leaf * LANES), 0) + start) == target
+            spread_ref[pl.ds(start, place_rows), :] = jnp.where(hit, 1.0, 0.0).astype(BF)
+
     def build_weights(which, source_ref):
-        wf_ref[which] = jnp.zeros(wf_ref.shape[1:], BF)
-        extra_shape = (HALF - rank, nm)
-        extra = (iota(extra_shape, 0) < 3) & (iota(extra_shape, 1) == mid_cols)
+        spread = dot(source_ref[...], spread_ref[...]).astype(BF)
+        shape = (nm - mid_cols, n_leaf * LANES)
+        cols = iota(shape, 1)
+        inner = cols % HALF
+        extra = (iota(shape, 0) == 0) & ((cols % LANES) // HALF == parity) & (inner >= rank) & (inner < rank + 3)
         extra = jnp.where(extra, 1.0, 0.0).astype(BF)
-        for l in range(n_leaf):
-            start = l * LANES + parity * HALF
-            wf_ref[which, pl.ds(pl.multiple_of(start, 16), rank), 0:mid_cols] = source_ref[l * rank:(l + 1) * rank, :]
-            wf_ref[which, pl.ds(pl.multiple_of(start + rank, 16), HALF - rank), :] = extra
-
-    def gram_pieces():
+        full = jnp.concatenate([spread, extra], axis=0)
+        wf_ref[which] = full
+
+    def build_gram():
         full = gall_ref[...].reshape(n_rows * rank, nm)
         full = jnp.concatenate([full, jnp.zeros((nm - n_rows * rank, nm), F32)], axis=0)
         hi = full.astype(BF)
-        return hi, (full - hi.astype(F32)).astype(BF)
+        gram_ref[0] = hi
+        gram_ref[1] = (full - hi.astype(F32)).astype(BF)
 
     def build_back(which):
-        hi, lo = gram_pieces()
-
-        @pl.loop(0, n_leaf * LANES // chunk)
-        def _(i):
-            start = pl.multiple_of(i * chunk, chunk)
-            part = wf_ref[which, pl.ds(start, chunk), :]
-            gwt_ref[which, pl.ds(start, chunk), :] = (dot(part, hi) + dot(part, lo)).astype(BF)
-
-    def apply(a, which, field, local_dot, first_window=None, last_window=None):
+        part = wf_ref[which]
+        wb_ref[which] = (dot(gram_ref[0], part) + dot(gram_ref[1], part)).astype(BF)
+
+    def apply(a, which, field, local_dot, windows=None):
         coeffs = dot(field.astype(BF), cpf_ref[...])
         tagged = lanes_of(local_dot)
         for j in range(pairs):
@@ -156,12 +164,12 @@
             copy.start()
             forward.append(copy)
         fr_ref[a, leaf] = fs_ref[a, leaf // 2]
-        if first_window is not None:
-            first_window()
+        if windows is not None:
+            windows[0]()
         for copy in forward:
             copy.wait_recv()
         incoming = jnp.concatenate([fr_ref[a, l] for l in range(n_leaf)], axis=1)
-        rr_ref[a, row] = dot(incoming, wf_ref[which])
+        rr_ref[a, row] = dot_t(incoming, wf_ref[which])
         across = []
         for d in range(1, n_rows):
             copy = pltpu.make_async_remote_copy(
@@ -171,15 +179,16 @@
             )
             copy.start()
             across.append(copy)
-        hi, lo = gram_pieces()
+        if windows is not None:
+            windows[1]()
         for copy in across:
             copy.wait_recv()
         totals = rr_ref[a, 0]
         for r in range(1, n_rows):
             totals = totals + rr_ref[a, r]
         head = totals.astype(BF)
-        back = dot_t(head, gwt_ref[which])
-        energy = jnp.sum(head.astype(F32) * (dot(head, hi) + dot(head, lo)), axis=1, keepdims=True)
+        back = dot(head, wb_ref[which])
+        energy = jnp.sum(head.astype(F32) * dot(head, gram_ref[0]), axis=1, keepdims=True)
         tagged = jnp.where(lane // HALF == parity, lanes_of(energy), 0.0)
         for l in range(n_leaf):
             bs_ref[a, l] = (back[:, l * LANES:(l + 1) * LANES] + tagged).astype(BF)
@@ -194,15 +203,15 @@
             copy.start()
             backward.append(copy)
         br_ref[a, leaf] = bs_ref[a, leaf]
-        if last_window is not None:
-            last_window()
+        if windows is not None:
+            windows[2]()
         for copy in backward:
             copy.wait_recv()
         tiles = [br_ref[a, 2 * j].astype(F32) + br_ref[a, 2 * j + 1].astype(F32) for j in range(pairs)]
         energies = functools.reduce(jnp.add, tiles)
         energies = jnp.where((inner_lane >= rank) & (inner_lane < rank + 3), energies, 0.0)
         arrived = jnp.concatenate(tiles, axis=1).astype(BF)
-        image = dot_t(arrived, cpf_ref[...])
+        image = dot(arrived, cpb_ref[...])
         total_dot = totals[:, mid_cols:mid_cols + 1] + jnp.sum(energies, axis=1, keepdims=True)
         waits.extend(forward + across + backward)
         return image, total_dot
@@ -210,18 +219,24 @@
     diagonal = diag_ref[...]
     residual = rhs_ref[...]
 
-    def prepare_first():
+    def first_window():
+        build_spread()
         build_weights(0, pre_ref)
+
+    def second_window():
         for copy in gram_copies:
             copy.wait_recv()
+        build_gram()
         build_back(0)
 
-    def prepare_second():
+    def third_window():
+        cpb_ref[...] = cpf_ref[...].T
         build_weights(1, mid_ref)
         build_back(1)
 
+    windows = (first_window, second_window, third_window)
     scaled = residual / diagonal
-    mapped, rz = apply(0, 0, residual, jnp.sum(residual * scaled, axis=1, keepdims=True), prepare_first, prepare_second)
+    mapped, rz = apply(0, 0, residual, jnp.sum(residual * scaled, axis=1, keepdims=True), windows)
     direction = scaled + mapped
     solution = jnp.zeros_like(residual)
     for iteration in range(ITERS):
@@ -244,7 +259,8 @@
 def per_device(n_leaf, n_rows, right_side, diagonal, tree_order, mid_perm, col_factor, mid_factor, pre_factor, row_factor):
     sides, points = right_side.shape
     rank = row_factor.shape[0]
-    mid_cols = mid_factor.shape[1]
+    mid_factor, pre_factor = mid_factor.T, pre_factor.T
+    mid_cols = mid_factor.shape[0]
     nm = (mid_cols // LANES + 1) * LANES
     pairs = n_leaf // 2
     applies = 2 * ITERS
@@ -262,9 +278,12 @@
             pltpu.VMEM((n_leaf * rank, pairs * LANES), BF),
             pltpu.VMEM((points, pairs * LANES), BF),
             pltpu.VMEM((points, pairs * LANES), BF),
-            pltpu.VMEM((2, n_leaf * LANES, nm), BF),
-            pltpu.VMEM((2, n_leaf * LANES, nm), BF),
+            pltpu.VMEM((pairs * LANES, points), BF),
+            pltpu.VMEM((n_leaf * rank, n_leaf * LANES), BF),
+            pltpu.VMEM((2, nm, n_leaf * LANES), BF),
+            pltpu.VMEM((2, nm, n_leaf * LANES), BF),
             pltpu.VMEM((n_rows, rank, nm), F32),
+            pltpu.VMEM((2, nm, nm), BF),
             pltpu.VMEM((applies, pairs, sides, LANES), BF),
             pltpu.VMEM((applies, n_leaf, sides, LANES), BF),
             pltpu.VMEM((applies, n_rows, sides, nm), F32),

time: 65.3 us -> 59.4 us (0.910)
  Pallas kernels: 59.8 us -> 56.6 us
  local copies, waits for them, and re-layouts: 4.58 us -> 2 us
    pallas_call x1, Pallas kernels: 59.8 us -> 56.6 us  [per_device(): pl.pallas_call(functools.partial(kernel, n_leaf, n_rows), out_shape=(jax....]
    unnamed x8 -> x4, local copies, waits for them, and re-layouts: 4.58 us -> 2 us
where the time goes in v2:
time: 59.4 us; the launch traced here: 59.2 us
  Pallas kernels  56.6 us (95%)
  local copies, waits for them, and re-layouts  2 us (3%)
  between operations  0.65 us (1%)
    pallas_call x1, Pallas kernels, per_device(): pl.pallas_call(functools.partial(kernel, n_leaf, n_rows), out_shape=(jax....  56.6 us
    unnamed x4, local copies, waits for them, and re-layouts  2 us

profile of v2, /device:TPU:0, one launch (start us, length us, event | category | flops | bytes accessed | tf_op | source)
XLA Modules:
  0.0 59.2 jit_solution(7041419577381049870)
XLA Ops:
  0.6 56.6 %shard_map.95 = (f32[8,1024]{1,0:T(8,128)}, f32[8,1024]{1,0:T(8,128)}) custom-call(f32[8,1024]{1,0:T(8,128)} %rhs_ref.1, f32[1,1024]{1,0:T(1,128)} %bitcast.6, s32[1,1024]{1,0:T(1,128)} %bitcast.7, s32[8]{0:T(128)} %perm_ref.1, bf16[1024,384]{1,0:T(8,128)(2,1)} %col_ref.1, bf16[192,384]{1,0:T(8,128)(2,1)} %bitcast.4, bf16[192,384]{1,0:T(8,128)(2,1)} %bitcast.5, ...), custom_call_target="tpu_custom_call" | custom-call | tf_op jit(solution)/shard_map/pallas_call | solution.py:269
  57.2 0.0 copy-start
  57.2 1.4 %copy.12 = f32[8,1024]{1,0:T(8,128)} copy(f32[8,1024]{1,0:T(8,128)} %get-tuple-element.4) | data formatting | bytes 65536
  58.6 0.0 copy-done
  58.6 0.6 %copy.13 = f32[8,1024]{1,0:T(8,128)} copy(f32[8,1024]{1,0:T(8,128)S(1)} %copy-done) | data formatting | bytes 65536
Async XLA Ops:
  57.2 1.4 %copy-start = (f32[8,1024]{1,0:T(8,128)S(1)}, f32[8,1024]{1,0:T(8,128)}, u32[]{:S(2)}) copy-start(f32[8,1024]{1,0:T(8,128)} %get-tuple-element.5) | copy-start | bytes 98308

commit v3 on v2

--- a/solution.py
+++ b/solution.py
@@ -35,9 +35,9 @@
 
 
 def kernel(
-    n_leaf, n_rows, rhs_ref, diag_ref, order_ref, perm_ref, col_ref, mid_ref, pre_ref, row_ref,
+    n_leaf, n_rows, rhs_ref, diag_ref, order_ref, perm_ref, col_hbm, mid_ref, pre_ref, row_ref,
     sol_ref, res_ref,
-    place_ref, colp_ref, cpf_ref, cpb_ref, spread_ref, wf_ref, wb_ref, gall_ref, gram_ref,
+    col_ref, col_sem, place_ref, colp_ref, cpf_ref, cpb_ref, spread_ref, wf_ref, wb_ref, gall_ref, gram_ref,
     fs_ref, fr_ref, rr_ref, bs_ref, br_ref,
     g_send, g_recv, f_send, f_recv, r_send, r_recv, b_send, b_recv,
 ):
@@ -52,6 +52,8 @@
     parity = lax.rem(leaf, 2)
     waits = []
 
+    col_copy = pltpu.make_async_copy(col_hbm, col_ref, col_sem)
+    col_copy.start()
     barrier = pltpu.get_barrier_semaphore()
     for d in range(1, n_leaf):
         pl.semaphore_signal(barrier, inc=1, device_id=(lax.rem(leaf + d, n_leaf), row), device_id_type=MESH)
@@ -80,6 +82,7 @@
         place_ref[pl.ds(start, place_rows), :] = jnp.where(hit, 1.0, 0.0).astype(BF)
 
     chunk = min(CHUNK, points)
+    col_copy.wait()
 
     @pl.loop(0, points // chunk)
     def _(i):
@@ -231,17 +234,17 @@
 
     def third_window():
         cpb_ref[...] = cpf_ref[...].T
-        build_weights(1, mid_ref)
-        build_back(1)
 
     windows = (first_window, second_window, third_window)
+    later_windows = (lambda: build_weights(1, mid_ref), lambda: build_back(1), lambda: None)
     scaled = residual / diagonal
     mapped, rz = apply(0, 0, residual, jnp.sum(residual * scaled, axis=1, keepdims=True), windows)
     direction = scaled + mapped
     solution = jnp.zeros_like(residual)
     for iteration in range(ITERS):
         scaled = diagonal * direction
-        mapped, curved = apply(2 * iteration + 1, 1, direction, jnp.sum(direction * scaled, axis=1, keepdims=True))
+        local_dot = jnp.sum(direction * scaled, axis=1, keepdims=True)
+        mapped, curved = apply(2 * iteration + 1, 1, direction, local_dot, later_windows if iteration == 0 else None)
         alpha = rz / curved
         solution = solution + alpha * direction
         residual = residual - alpha * (scaled + mapped)
@@ -272,9 +275,11 @@
             jax.ShapeDtypeStruct((sides, points), F32),
             jax.ShapeDtypeStruct((sides, points), F32),
         ),
-        in_specs=[vmem, vmem, vmem, pl.BlockSpec(memory_space=pltpu.SMEM), vmem, vmem, vmem, vmem],
+        in_specs=[vmem, vmem, vmem, pl.BlockSpec(memory_space=pltpu.SMEM), pl.BlockSpec(memory_space=pl.ANY), vmem, vmem, vmem],
         out_specs=(vmem, vmem),
         scratch_shapes=[
+            pltpu.VMEM(col_factor.shape, BF),
+            dma,
             pltpu.VMEM((n_leaf * rank, pairs * LANES), BF),
             pltpu.VMEM((points, pairs * LANES), BF),
             pltpu.VMEM((points, pairs * LANES), BF),

time: 59.4 us -> 59.4 us (level)
  no operation moved by 1% of the time
where the time goes in v3:
time: 59.4 us; the launch traced here: 59.2 us
  Pallas kernels  56.5 us (95%)
  local copies, waits for them, and re-layouts  2 us (3%)
  between operations  0.65 us (1%)
    pallas_call x1, Pallas kernels, per_device(): pl.pallas_call(functools.partial(kernel, n_leaf, n_rows), out_shape=(jax....  56.5 us
    unnamed x4, local copies, waits for them, and re-layouts  2 us

profile of v3, /device:TPU:0, one launch (start us, length us, event | category | flops | bytes accessed | tf_op | source)
XLA Modules:
  0.0 59.2 jit_solution(17670961859485497213)
XLA Ops:
  0.6 56.5 %shard_map.95 = (f32[8,1024]{1,0:T(8,128)}, f32[8,1024]{1,0:T(8,128)}) custom-call(f32[8,1024]{1,0:T(8,128)} %rhs_ref.1, f32[1,1024]{1,0:T(1,128)} %bitcast.6, s32[1,1024]{1,0:T(1,128)} %bitcast.7, s32[8]{0:T(128)} %perm_ref.1, bf16[1024,384]{1,0:T(8,128)(2,1)} %col_hbm.1, bf16[192,384]{1,0:T(8,128)(2,1)} %bitcast.4, bf16[192,384]{1,0:T(8,128)(2,1)} %bitcast.5, ...), custom_call_target="tpu_custom_call" | custom-call | tf_op jit(solution)/shard_map/pallas_call | solution.py:272
  57.2 0.0 copy-start
  57.2 1.4 %copy.12 = f32[8,1024]{1,0:T(8,128)} copy(f32[8,1024]{1,0:T(8,128)} %get-tuple-element.4) | data formatting | bytes 65536
  58.6 0.0 copy-done
  58.6 0.6 %copy.13 = f32[8,1024]{1,0:T(8,128)} copy(f32[8,1024]{1,0:T(8,128)S(1)} %copy-done) | data formatting | bytes 65536
Async XLA Ops:
  57.2 1.4 %copy-start = (f32[8,1024]{1,0:T(8,128)S(1)}, f32[8,1024]{1,0:T(8,128)}, u32[]{:S(2)}) copy-start(f32[8,1024]{1,0:T(8,128)} %get-tuple-element.5) | copy-start | bytes 98308
